TPU v7x, 32 devices: a whole 2x2x4 slice. The times are simulated.
32 devices in a mesh: groups: 2 (over x), seq: 16 (over z, y, core).
Axes of the slice: x: 2, y: 2, z: 4, core: 2. Of those that a mesh axis runs over, the one named last changes fastest.
Arguments:
- queries: bfloat16 [8192, 4096], P(('groups', 'seq')), parts along dimension 0, may hold values from -13 to 13
- keys: bfloat16 [8192, 512], P(('groups', 'seq')), parts along dimension 0, may hold values from -13 to 13
- values: bfloat16 [8192, 512], P(('groups', 'seq')), parts along dimension 0, may hold values from -6 to 6
- segment_ids: int32 [8192], P(('groups', 'seq')), parts along dimension 0, may hold values from 0 to 8, as said below
Outputs:
- attended: bfloat16 [8192, 4096], P(('groups', 'seq')), parts along dimension 0
- rotated_keys: bfloat16 [8192, 512], P(('groups', 'seq')), parts along dimension 0
There are 2 independent parts, one for each index of `groups`. A program takes and returns all parts, laid end to end along the dimension named above; each array names one. Nothing has to cross between parts.
Inputs may be any that keep to these rules, and one draw needn't show every extreme that they name: `segment_ids`: never falling along the packed stream, starting at 0 and rising by one at each new rollout; each rollout covers 1 to 1792 tokens and one covers exactly 1792.
All inputs are finite; a program needn't handle non-finite values.
Results may differ from a plain program's by a relative error of at most 0.0054.
Values may be sent and summed in bfloat16 or wider, within the bound.
A program may use at most 192 MiB of HBM per device.

v0:
```python
from functools import partial

import jax
import jax.numpy as jnp
from jax import lax
from jax.experimental import pallas as pl
from jax.experimental.pallas import tpu as pltpu
from jax.sharding import PartitionSpec as P

HD = 128
SPAN = 7
ROPE_BASE = 1000000.0
BIG = 1e30
NO_SEGMENT = 127
LANES = 128
ONES_ROWS = 16
SEG_ROWS = 16
PIECES = 4


def tables(positions):
    half_dim = HD // 2
    inverse_freq = ROPE_BASE ** (-(jnp.arange(half_dim, dtype=jnp.float32) * (2.0 / HD)))
    angles = positions.astype(jnp.float32)[:, None] * inverse_freq[None, :]
    cosine, sine = jnp.cos(angles), jnp.sin(angles)
    return (
        jnp.concatenate([cosine, cosine], axis=-1),
        jnp.concatenate([-sine, sine], axis=-1),
    )


def rotate_heads(matrix, cosine, sine):
    rows, width = matrix.shape
    heads = matrix.astype(jnp.float32).reshape(rows, width // HD, HD)
    swapped = jnp.concatenate([heads[..., HD // 2 :], heads[..., : HD // 2]], axis=-1)
    turned = heads * cosine[:, None, :] + swapped * sine[:, None, :]
    return turned.reshape(rows, width).astype(jnp.bfloat16)


def one_hot(segment_row):
    rows = lax.broadcasted_iota(jnp.int32, (LANES, segment_row.shape[1]), 0).astype(jnp.float32)
    return jnp.where(rows == segment_row, 1.0, 0.0).T


def attend_phase(slots, head, group, qa, qhot, block, khot, vt, top, acc, causal):
    first = causal is not None
    rows = qhot.shape[0]
    query = jnp.concatenate([qa[head], qhot[...]], axis=1)
    kv = head // group
    at = pl.ds(pl.multiple_of(SEG_ROWS + kv * rows, SEG_ROWS), rows)
    parts = []
    for slot in slots:
        key = jnp.concatenate([block(slot)[at, :HD], khot[slot]], axis=1)
        part = lax.dot_general(
            key, query, (((1,), (1,)), ((), ())), preferred_element_type=jnp.float32
        )
        parts.append(part + causal[...] if first else part)
    new_top = jnp.max(parts[0], axis=0, keepdims=True)
    for part in parts[1:]:
        new_top = jnp.maximum(new_top, jnp.max(part, axis=0, keepdims=True))
    if not first:
        old_top = top[head]
        new_top = jnp.maximum(new_top, old_top)
    mixed = None
    for slot, part in zip(slots, parts):
        weights = jnp.exp2(part - new_top).astype(jnp.bfloat16)
        term = jnp.dot(vt[slot, kv], weights, preferred_element_type=jnp.float32)
        mixed = term if mixed is None else mixed + term
    if not first:
        mixed = mixed + acc[head] * jnp.exp2(old_top - new_top)
    return new_top, mixed


def kernel(
    group, count, q_ref, cos_ref, sin_ref, own_ref, keys_ref, freq_ref, out_ref, rot_ref,
    recv, qa, qhot, khot, vt, top, acc, causal, send_sems, recv_sems,
):
    rows = q_ref.shape[0]
    heads = q_ref.shape[1] // HD
    kv_heads = heads // group
    me = lax.axis_index("seq")
    core = lax.rem(me, 2)
    side = lax.rem(me // 2, 2)
    plane = me // 4
    planes = count // 4
    partner = me + 1 - 2 * core
    across = me + 2 - 4 * side
    ahead = me + 4
    behind = me - 4
    has_ahead = plane + 1 < planes
    has_behind = plane >= 1

    def block(slot):
        return own_ref if slot == 0 else recv.at[slot]

    def chunk(piece):
        if piece == 0:
            return pl.ds(0, SEG_ROWS + rows)
        return pl.ds(SEG_ROWS + piece * rows, rows)

    barrier = pltpu.get_barrier_semaphore()

    def greet(device):
        pl.semaphore_signal(
            barrier, inc=1, device_id={"seq": device}, device_id_type=pl.DeviceIdType.MESH
        )

    greet(partner)
    greet(across)

    @pl.when(has_ahead)
    def _():
        greet(ahead)

    @pl.when(has_behind)
    def _():
        greet(behind)

    both = has_ahead & has_behind
    one = (has_ahead | has_behind) & jnp.logical_not(both)
    neither = jnp.logical_not(has_ahead | has_behind)
    for extra, condition in ((2, both), (1, one), (0, neither)):

        @pl.when(condition)
        def _():
            pl.semaphore_wait(barrier, 2 + extra)

    sent = []

    def copy(kind, piece, source, distance, device):
        src = own_ref if source is None else recv.at[source]
        return pltpu.make_async_remote_copy(
            src_ref=src.at[chunk(piece)],
            dst_ref=recv.at[distance, chunk(piece)],
            send_sem=send_sems.at[kind, piece],
            recv_sem=recv_sems.at[distance, piece],
            device_id={"seq": device},
            device_id_type=pl.DeviceIdType.MESH,
        )

    def send(condition, *what):
        @pl.when(condition)
        def _():
            copy(*what).start()

        sent.append((condition, what))

    def arrive(condition, distance, piece):
        @pl.when(condition)
        def _():
            copy(0, piece, None, distance, partner).wait_recv()

    to_partner = 1 - 2 * core
    has_two = (side == 1) | (plane >= 1)
    has_six = ((side == 1) & (plane >= 1)) | (plane >= 2)
    relays = (side == 1) | (core == 1)
    has_eight = (plane >= 2) & relays
    for piece in range(PIECES):
        send(has_ahead, 0, piece, None, 4, ahead)
        send(side == 0, 1, piece, None, 2, across)
        send(core == 0, 2, piece, None, 1, partner)

    def near(point):
        if point < PIECES:
            arrive(has_behind, 4, point)
            send(has_behind, 3, point, 4, 6 - 4 * side, across)
            send(has_behind & has_ahead & relays, 4, point, 4, 8, ahead)
            send(has_behind, 5, point, 4, 4 + to_partner, partner)
        if point > 0:
            arrive(has_two, 2, point - 1)
            send(has_two, 6, point - 1, 2, 2 + to_partner, partner)

    def far(point):
        if point < PIECES:
            arrive(has_eight, 8, point)
            send(has_eight & (side == 1), 7, point, 8, 6, across)
            send(has_eight & (core == 1), 8, point, 8, 7, partner)
        if point > 0:
            arrive(has_six, 6, point - 1)
            send(has_six, 9, point - 1, 6, 6 + to_partner, partner)

    filler = jnp.full((SEG_ROWS, 2 * HD), NO_SEGMENT, jnp.bfloat16)
    for distance in range(1, SPAN + 1):

        @pl.when(me < distance)
        def _():
            recv[distance, :SEG_ROWS, :] = filler
            recv[distance, SEG_ROWS:, :] = jnp.zeros((kv_heads * rows, 2 * HD), jnp.bfloat16)

    scale = HD ** (-0.5) * 1.4426950408889634
    cosine = cos_ref[...] * scale
    sine = sin_ref[...] * scale

    def turn(head, carry):
        columns = pl.ds(pl.multiple_of(head * HD, HD), HD)
        x = q_ref[:, columns].astype(jnp.float32)
        qa[head] = (x * cosine + pltpu.roll(x, HD // 2, 1) * sine).astype(jnp.bfloat16)
        return carry

    lax.fori_loop(0, heads, turn, 0)

    def segment_row(slot):
        return block(slot)[:SEG_ROWS, :].astype(jnp.float32)[:1]

    qhot[...] = ((one_hot(segment_row(0)) - 1.0) * BIG).astype(jnp.bfloat16)
    key_at = lax.broadcasted_iota(jnp.int32, (rows, rows), 0)
    query_at = lax.broadcasted_iota(jnp.int32, (rows, rows), 1)
    causal[...] = jnp.where(key_at <= query_at, 0.0, -BIG)

    def prepare(slots):
        for slot in slots:
            khot[slot] = one_hot(segment_row(slot)).astype(jnp.bfloat16)

            def flip(kv, carry):
                at = pl.ds(pl.multiple_of(SEG_ROWS + kv * rows, SEG_ROWS), rows)
                flipped = block(slot)[at, HD:].astype(jnp.float32).T
                vt[slot, kv, :HD, :] = flipped.astype(jnp.bfloat16)
                vt[slot, kv, HD:, :] = jnp.ones((ONES_ROWS, rows), jnp.bfloat16)
                return carry

            lax.fori_loop(0, kv_heads, flip, 0)

    def attend(slots, low, high, first, last):
        def step(index, carry):
            for head in (2 * index, 2 * index + 1):
                new_top, mixed = attend_phase(
                    slots, head, group, qa, qhot, block, khot, vt, top, acc,
                    causal if first else None,
                )
                if last:
                    columns = pl.ds(pl.multiple_of(head * HD, HD), HD)
                    result = mixed[:HD] * (1.0 / mixed[HD : HD + 1])
                    out_ref[:, columns] = result.T.astype(jnp.bfloat16)
                else:
                    top[head] = new_top
                    acc[head] = mixed
            return carry

        lax.fori_loop(low // 2, high // 2, step, 0)

    part = heads // PIECES
    prepare((0,))
    for piece in range(PIECES):
        near(piece)
        attend((0,), piece * part, (piece + 1) * part, True, False)
    near(PIECES)
    for piece in range(PIECES):
        arrive(me >= 1, 1, piece)
        arrive(me >= 3, 3, piece)
    prepare((1, 2, 3, 4))
    for piece in range(PIECES):
        far(piece)
        attend((1, 2, 3, 4), piece * part, (piece + 1) * part, False, False)
    far(PIECES)
    for piece in range(PIECES):
        arrive(me >= 5, 5, piece)
        arrive(me >= 7, 7, piece)
    prepare((5, 6, 7))
    attend((5, 6, 7), 0, heads, False, True)

    mine = segment_row(0)
    lead = mine[:, :1]
    earlier = jnp.zeros((1, 1), jnp.float32)
    for distance in range(1, SPAN + 1):
        same = jnp.where(segment_row(distance) == lead, 1.0, 0.0)
        earlier = earlier + jnp.sum(same, axis=1, keepdims=True)
    column = jnp.broadcast_to(mine, (LANES, rows)).T[:, :1]
    before = jnp.sum(jnp.where(mine < column, 1.0, 0.0), axis=1, keepdims=True)
    index = lax.broadcasted_iota(jnp.int32, (rows, 1), 0).astype(jnp.float32)
    positions = index - before + jnp.where(column == lead, earlier, 0.0)
    angles = positions * freq_ref[...]
    lane = lax.broadcasted_iota(jnp.int32, (rows, HD), 1)
    cosine = jnp.cos(angles)
    sine = jnp.where(lane < HD // 2, -1.0, 1.0) * jnp.sin(angles)
    for kv in range(kv_heads):
        x = keys_ref[:, kv * HD : (kv + 1) * HD].astype(jnp.float32)
        turned = x * cosine + pltpu.roll(x, HD // 2, 1) * sine
        rot_ref[:, kv * HD : (kv + 1) * HD] = turned.astype(jnp.bfloat16)

    for condition, what in sent:

        @pl.when(condition)
        def _():
            copy(*what).wait_send()


def local(queries, keys, values, segment_ids):
    rows = queries.shape[0]
    heads = queries.shape[1] // HD
    kv_heads = keys.shape[1] // HD
    count = lax.axis_size("seq")
    row_index = lax.axis_index("seq") * rows + jnp.arange(rows, dtype=jnp.int32)
    cosine, sine = tables(row_index)
    turned = rotate_heads(keys, cosine, sine)
    segment_rows = jnp.broadcast_to(segment_ids.astype(jnp.bfloat16)[None], (SEG_ROWS, rows))
    pieces = [segment_rows]
    for kv in range(kv_heads):
        part = slice(kv * HD, (kv + 1) * HD)
        pieces.append(jnp.concatenate([turned[:, part], values[:, part]], axis=1))
    own = jnp.concatenate(pieces, axis=0)
    inverse_freq = ROPE_BASE ** (-(jnp.arange(HD // 2, dtype=jnp.float32) * (2.0 / HD)))
    frequencies = jnp.concatenate([inverse_freq, inverse_freq])[None]
    vmem = pl.BlockSpec(memory_space=pltpu.VMEM)
    slots = SPAN + 2
    return pl.pallas_call(
        partial(kernel, heads // kv_heads, count),
        out_shape=(
            jax.ShapeDtypeStruct(queries.shape, jnp.bfloat16),
            jax.ShapeDtypeStruct(keys.shape, jnp.bfloat16),
        ),
        in_specs=[vmem] * 6,
        out_specs=(vmem, vmem),
        scratch_shapes=[
            pltpu.VMEM((slots, *own.shape), jnp.bfloat16),
            pltpu.VMEM((heads, rows, HD), jnp.bfloat16),
            pltpu.VMEM((rows, LANES), jnp.bfloat16),
            pltpu.VMEM((slots, rows, LANES), jnp.bfloat16),
            pltpu.VMEM((slots, kv_heads, HD + ONES_ROWS, rows), jnp.bfloat16),
            pltpu.VMEM((heads, 1, rows), jnp.float32),
            pltpu.VMEM((heads, HD + ONES_ROWS, rows), jnp.float32),
            pltpu.VMEM((rows, rows), jnp.float32),
            pltpu.SemaphoreType.DMA((10, PIECES)),
            pltpu.SemaphoreType.DMA((slots, PIECES)),
        ],
        compiler_params=pltpu.CompilerParams(
            vmem_limit_bytes=60 * 1024 * 1024, collective_id=0, has_side_effects=True
        ),
    )(queries, cosine, sine, own, keys, frequencies)


def solution(mesh):
    in_specs = (
        P(("groups", "seq"), None),
        P(("groups", "seq"), None),
        P(("groups", "seq"), None),
        P(("groups", "seq")),
    )
    out_specs = (P(("groups", "seq"), None), P(("groups", "seq"), None))
    return jax.shard_map(local, mesh=mesh, in_specs=in_specs, out_specs=out_specs, check_vma=False)
```

profile of v0, /device:TPU:17, one launch (start us, length us, event | category | flops | bytes accessed | tf_op | source)
XLA Modules:
  0.0 82.9 jit_solution(792085076335961812)
XLA Ops:
  0.6 0.0 copy-start
  0.7 0.6 maximum_bitcast_fusion.freq_ref
  1.3 0.7 convert_element_type.17
  2.0 1.0 %fusion.4 = (bf16[256,128]{1,0:T(8,128)(2,1)S(1)}, bf16[256,128]{1,0:T(8,128)(2,1)S(1)}, bf16[256,128]{1,0:T(8,128)(2,1)S(1)}, bf16[256,128]{1,0:T(8,128)(2,1)S(1)}) fusion(bf16[256,512]{1,0:T(8,128)(2,1)} %param.6), kind=kLoop, calls=%fused_computation.19 | loop fusion | bytes 524288 | tf_op jit(solution)/shard_map/slice | solution.py:299
  3.0 0.5 fusion.1
  3.5 0.1 pad_maximum_fusion
  3.6 0.0 copy-start.1
  3.7 0.0 copy-start.2
  3.7 0.1 mul.56
  3.8 0.0 copy-done
  3.8 0.2 reshape.26
  3.9 0.3 fusion.2
  4.3 0.4 maximum_multiply_fusion
  4.6 0.0 copy-done.1
  4.7 0.0 copy-done.2
  4.7 0.1 fusion
  5.0 0.0 copy-start.3
  5.0 0.8 copy-done.3
  5.8 73.3 %shard_map.59 = (bf16[256,4096]{1,0:T(8,128)(2,1)}, bf16[256,512]{1,0:T(8,128)(2,1)}) custom-call(bf16[256,4096]{1,0:T(8,128)(2,1)} %q_ref.1, f32[256,128]{1,0:T(8,128)} %copy-done.1, f32[256,128]{1,0:T(8,128)} %copy-done.2, bf16[1040,256]{1,0:T(8,128)(2,1)} %copy-done.3, bf16[256,512]{1,0:T(8,128)(2,1)} %keys_ref.1, f32[1,128]{1,0:T(1,128)} %maximum_bitcast_fusion.freq_ref), custom_call_target="tpu_custom_call" | custom-call | tf_op jit(solution)/shard_map/pallas_call | solution.py:305
  79.0 0.0 copy-start.4
  79.1 3.2 %copy.16 = bf16[256,4096]{1,0:T(8,128)(2,1)} copy(bf16[256,4096]{1,0:T(8,128)(2,1)} %get-tuple-element.19) | data formatting | bytes 4194304
  82.2 0.0 copy-done.4
  82.2 0.7 copy.17
  (8 shorter events, 0.1 us)
Async XLA Ops:
  0.6 3.1 %copy-start = (bf16[256,512]{1,0:T(8,128)(2,1)S(1)}, bf16[256,512]{1,0:T(8,128)(2,1)}, u32[]{:S(2)}) copy-start(bf16[256,512]{1,0:T(8,128)(2,1)} %keys_ref.1) | copy-start | bytes 786436
  3.6 1.0 %copy-start.1 = (f32[256,128]{1,0:T(8,128)}, f32[256,128]{1,0:T(8,128)S(1)}, u32[]{:S(2)}) copy-start(f32[256,128]{1,0:T(8,128)S(1)} %get-tuple-element.15.cos_ref) | copy-start | bytes 393220
  3.7 1.0 %copy-start.2 = (f32[256,128]{1,0:T(8,128)}, f32[256,128]{1,0:T(8,128)S(1)}, u32[]{:S(2)}) copy-start(f32[256,128]{1,0:T(8,128)S(1)} %get-tuple-element.16.sin_ref) | copy-start | bytes 393220
  5.0 0.8 copy-start.3
  79.0 3.2 %copy-start.4 = (bf16[256,512]{1,0:T(8,128)(2,1)S(1)}, bf16[256,512]{1,0:T(8,128)(2,1)}, u32[]{:S(2)}) copy-start(bf16[256,512]{1,0:T(8,128)(2,1)} %get-tuple-element.20) | copy-start | bytes 786436
where the time goes:
time: 84.3 us; the launch traced here: 82.9 us
  Pallas kernels  73.3 us (87%)
  local copies, waits for them, and re-layouts  6.29 us (7%)
  other arithmetic  2.59 us (3%)
    pallas_call x1, Pallas kernels, local(): pl.pallas_call(partial(kernel, heads // kv_heads, count), out_shape=(jax....  73.3 us
    unnamed x13, local copies, waits for them, and re-layouts  4.69 us

commit v1 on v0

v1 whole, which is shorter than its diff:
```python
from functools import partial

import jax
import jax.numpy as jnp
import numpy as np
from jax import lax
from jax.experimental import pallas as pl
from jax.experimental.pallas import tpu as pltpu
from jax.sharding import PartitionSpec as P

HD = 128
HALF = HD // 2
SPAN = 7
ROPE_BASE = 1000000.0
BIG = 1e30
NO_SEGMENT = -1
ONES_ROWS = 16
STEP = 16
SLOTS = SPAN + 2
LOG2E = 1.4426950408889634


def kernel(
    kv_heads, count, q_hbm, k_hbm, v_hbm, seg_hbm, freq_ref, out_ref, rot_ref,
    kraw, vraw, segs, qraw, qa, qext, krot, kext, vt, ctab, stab, mask, scores_a, scores_b,
    top, acc, local_sems, send_sems, recv_sems, seg_send, seg_recv,
):
    rows = kraw.shape[1]
    heads = qa.shape[0]
    group = heads // kv_heads
    me = lax.axis_index("seq")
    core = lax.rem(me, 2)
    side = lax.rem(me // 2, 2)
    plane = me // 4
    planes = count // 4
    partner = me + 1 - 2 * core
    across = me + 2 - 4 * side
    ahead = me + 4
    behind = me - 4
    has_ahead = plane + 1 < planes
    has_behind = plane >= 1

    barrier = pltpu.get_barrier_semaphore()

    def greet(device):
        pl.semaphore_signal(
            barrier, inc=1, device_id={"seq": device}, device_id_type=pl.DeviceIdType.MESH
        )

    greet(partner)
    greet(across)

    @pl.when(has_ahead)
    def _():
        greet(ahead)

    @pl.when(has_behind)
    def _():
        greet(behind)

    def columns(kv):
        return pl.ds(pl.multiple_of(kv * HD, HD), HD)

    def load(index, src, dst):
        return pltpu.make_async_copy(src, dst, local_sems.at[index])

    seg_load = load(0, seg_hbm, segs.at[0])
    seg_load.start()
    loads = []
    for kv in range(kv_heads):
        at = slice(kv * HD, (kv + 1) * HD)
        loads.append((
            load(1 + 2 * kv, k_hbm.at[:, at], kraw.at[0, :, at]),
            load(2 + 2 * kv, v_hbm.at[:, at], vraw.at[0, :, at]),
        ))
        for one in loads[-1]:
            one.start()
    wide = group * HD
    q_loads = []
    for kv in range(kv_heads):
        at = slice(kv * wide, (kv + 1) * wide)
        q_loads.append(load(1 + 2 * kv_heads + kv, q_hbm.at[:, at], qraw.at[:, at]))
        q_loads[-1].start()

    both = has_ahead & has_behind
    one_side = (has_ahead | has_behind) & jnp.logical_not(both)
    neither = jnp.logical_not(has_ahead | has_behind)
    for extra, condition in ((2, both), (1, one_side), (0, neither)):

        @pl.when(condition)
        def _():
            pl.semaphore_wait(barrier, 2 + extra)

    def piece_copy(kind, half, kv, source, distance, device):
        buffer = (kraw, vraw)[half]
        return pltpu.make_async_remote_copy(
            src_ref=buffer.at[source, :, columns(kv)],
            dst_ref=buffer.at[distance, :, columns(kv)],
            send_sem=send_sems.at[kind, kv, half],
            recv_sem=recv_sems.at[distance, kv, half],
            device_id={"seq": device},
            device_id_type=pl.DeviceIdType.MESH,
        )

    def seg_copy(kind, source, distance, device):
        return pltpu.make_async_remote_copy(
            src_ref=segs.at[source],
            dst_ref=segs.at[distance],
            send_sem=seg_send.at[kind],
            recv_sem=seg_recv.at[distance],
            device_id={"seq": device},
            device_id_type=pl.DeviceIdType.MESH,
        )

    to_partner = 1 - 2 * core
    relays = core == 1
    has_two = (side == 1) | has_behind
    has_six = ((side == 1) & has_behind) | (plane >= 2)
    has_eight = (plane >= 2) & relays
    flows = {
        0: (has_ahead, 0, 4, ahead),
        1: (side == 0, 0, 2, across),
        2: (core == 0, 0, 1, partner),
        3: (has_behind, 4, 6 - 4 * side, across),
        4: (has_behind & has_ahead & relays, 4, 8, ahead),
        5: (has_behind, 4, 4 + to_partner, partner),
        6: (has_two, 2, 2 + to_partner, partner),
        7: (has_eight & (side == 1), 8, 6, across),
        8: (has_eight, 8, 7, partner),
        9: (has_six, 6, 6 + to_partner, partner),
        10: ((side == 0) & (core == 0) & has_behind & has_ahead, 2, 6, ahead),
    }

    def send(kinds, half, kv):
        for kind in kinds:
            condition, source, distance, device = flows[kind]

            @pl.when(condition)
            def _():
                piece_copy(kind, half, kv, source, distance, device).start()

    def send_segs(kinds):
        for kind in kinds:
            condition, source, distance, device = flows[kind]

            @pl.when(condition)
            def _():
                seg_copy(kind, source, distance, device).start()

    def arrive(condition, distance, half, kv):
        @pl.when(condition)
        def _():
            piece_copy(0, half, kv, 0, distance, partner).wait_recv()

    def arrive_segs(condition, distance):
        @pl.when(condition)
        def _():
            seg_copy(0, 0, distance, partner).wait_recv()

    def relay(condition, distance, kinds, kv):
        for half in range(2):
            arrive(condition, distance, half, kv)
            send(kinds, half, kv)

    def relay_segs(condition, distance, kinds):
        arrive_segs(condition, distance)
        send_segs(kinds)

    seg_load.wait()
    send_segs((0, 1, 2))
    for kv in range(kv_heads):
        for half in range(2):
            loads[kv][half].wait()
            send((0, 1, 2), half, kv)

    for distance in range(1, SPAN + 1):

        @pl.when(me < distance)
        def _():
            segs[distance] = jnp.full(segs.shape[1:], NO_SEGMENT, jnp.int32)
            kraw[distance] = jnp.zeros(kraw.shape[1:], jnp.bfloat16)
            vraw[distance] = jnp.zeros(vraw.shape[1:], jnp.bfloat16)

    freq = freq_ref[...]
    lane = lax.broadcasted_iota(jnp.int32, (1, HD), 1)
    sign = jnp.where(lane < HALF, -1.0, 1.0)

    def fan(steps, stride):
        index = lax.broadcasted_iota(jnp.int32, (steps, HD), 0).astype(jnp.float32)
        angles = index * stride * freq
        return jnp.cos(angles), jnp.sin(angles)

    fine_c, fine_s = fan(STEP, 1.0)
    coarse_c, coarse_s = fan(rows // STEP, float(STEP))
    block_c, block_s = fan(SPAN + 1, float(rows))
    for i in range(rows // STEP):
        at = slice(i * STEP, (i + 1) * STEP)
        c, s = coarse_c[i : i + 1], coarse_s[i : i + 1]
        ctab[0, at, :] = fine_c * c - fine_s * s
        stab[0, at, :] = fine_s * c + fine_c * s
    base_c, base_s = ctab[0], stab[0]
    for d in range(1, SPAN + 1):
        c, s = block_c[d : d + 1], block_s[d : d + 1]
        ctab[d] = base_c * c + base_s * s
        stab[d] = (base_s * c - base_c * s) * sign
    stab[0] = base_s * sign

    scale = HD ** (-0.5) * LOG2E

    for one in q_loads:
        one.wait()

    def turn(head, carry):
        x = qraw[:, columns(head)].astype(jnp.float32)
        turned = x * (ctab[0] * scale) + pltpu.roll(x, HALF, 1) * (stab[0] * scale)
        qa[head] = turned.astype(jnp.bfloat16)
        return carry

    lax.fori_loop(0, heads, turn, 0, unroll=4)

    def seg_row(slot):
        return segs[slot].astype(jnp.float32)

    mine = seg_row(0)
    lead = mine[:, :1]
    row_at = lax.broadcasted_iota(jnp.int32, (HD, rows), 0)
    lane_at = lax.broadcasted_iota(jnp.int32, (rows, HD), 1)
    column = jnp.broadcast_to(mine, (HD, rows)).T[:, :1]
    barred = jnp.where(column == lead, 0.0, -BIG)
    ones_lane = jnp.where((lane_at >= 1) & (lane_at <= SPAN), 1.0, 0.0)
    qext[...] = jnp.where(lane_at == 0, barred, ones_lane).astype(jnp.bfloat16)
    key_at = lax.broadcasted_iota(jnp.int32, (rows, rows), 0)
    query_at = lax.broadcasted_iota(jnp.int32, (rows, rows), 1)
    mask[...] = jnp.where((key_at <= query_at) & (column == mine), 0.0, -BIG)

    for kv in range(kv_heads):
        vt[kv, HD:, :] = jnp.ones((ONES_ROWS, vt.shape[2]), jnp.bfloat16)

    def key_masks(slots):
        flat = jnp.where(row_at == 0, 1.0, 0.0)
        for slot in slots:
            bias = jnp.where(seg_row(slot) == lead, 0.0, -BIG)
            flat = jnp.where(row_at == slot, bias, flat)
        turned = flat.T
        for slot in slots:
            keep = (lane_at == 0) | (lane_at == slot)
            kext[slot] = jnp.where(keep, turned, 0.0).astype(jnp.bfloat16)

    def prepare(slots, kv):
        for slot in slots:
            x = kraw[slot, :, columns(kv)].astype(jnp.float32)
            turned = x * ctab[slot] + pltpu.roll(x, HALF, 1) * stab[slot]
            krot[kv, slot] = turned.astype(jnp.bfloat16)
            flipped = vraw[slot, :, columns(kv)].astype(jnp.float32).T
            vt[kv, :HD, slot * rows : (slot + 1) * rows] = flipped.astype(jnp.bfloat16)

    def attend(slots, kv, first, last):
        tops = {}

        def score(head, buffer):
            query = qa[head]
            if not first:
                query = jnp.concatenate([query, qext[...]], axis=1)
            best = None
            for i, slot in enumerate(slots):
                key = krot[kv, slot]
                if not first:
                    key = jnp.concatenate([key, kext[slot]], axis=1)
                part = lax.dot_general(
                    key, query, (((1,), (1,)), ((), ())), preferred_element_type=jnp.float32
                )
                if first:
                    part = part + mask[...]
                buffer[i * rows : (i + 1) * rows, :] = part
                high = jnp.max(part.reshape(rows // 8, 8, rows), axis=0)
                best = high if best is None else jnp.maximum(best, high)
            return jnp.max(best, axis=0, keepdims=True)

        def weigh(head, buffer, new_top):
            if not first:
                old_top = top[head]
                new_top = jnp.maximum(new_top, old_top)
            mixed = None
            for i, slot in enumerate(slots):
                part = buffer[i * rows : (i + 1) * rows, :]
                weights = jnp.exp2(part - new_top).astype(jnp.bfloat16)
                at = slice(slot * rows, (slot + 1) * rows)
                term = jnp.dot(vt[kv, :, at], weights, preferred_element_type=jnp.float32)
                mixed = term if mixed is None else mixed + term
            if not first:
                mixed = mixed + acc[head] * jnp.exp2(old_top - new_top)
            if last:
                result = mixed[:HD] * (1.0 / mixed[HD : HD + 1])
                out_ref[:, columns(head)] = result.T.astype(jnp.bfloat16)
            else:
                top[head] = new_top
                acc[head] = mixed

        buffers = (scores_a, scores_b)
        tops[0] = score(kv * group, buffers[0])
        for i in range(group):
            if i + 1 < group:
                tops[i + 1] = score(kv * group + i + 1, buffers[(i + 1) % 2])
            weigh(kv * group + i, buffers[i % 2], tops[i])

    near_slots = (1, 2, 3, 4)
    far_slots = (5, 6, 7)

    def own_phase(kv, carry):
        prepare((0,), kv)
        attend((0,), kv, True, False)
        return carry

    lax.fori_loop(0, kv_heads, own_phase, 0)

    relay_segs(has_behind, 4, (3, 4, 5))
    relay(has_behind, 4, (3, 4, 5), 0)
    relay_segs(has_two, 2, (6, 10))
    arrive_segs(me >= 1, 1)
    arrive_segs(me >= 3, 3)
    key_masks(near_slots)

    def near_phase(kv, carry):
        @pl.when(kv + 1 < kv_heads)
        def _():
            relay(has_behind, 4, (3, 4, 5), kv + 1)

        relay(has_two, 2, (6, 10), kv)
        for half in range(2):
            arrive(me >= 1, 1, half, kv)
            arrive(me >= 3, 3, half, kv)
        prepare(near_slots, kv)
        attend(near_slots, kv, False, False)
        return carry

    lax.fori_loop(0, kv_heads, near_phase, 0)

    relay_segs(has_eight, 8, (7, 8))
    relay(has_eight, 8, (7, 8), 0)
    relay_segs(has_six, 6, (9,))
    arrive_segs(me >= 5, 5)
    arrive_segs(me >= 7, 7)
    key_masks(far_slots)

    earlier = jnp.zeros((1, 1), jnp.float32)
    for distance in range(1, SPAN + 1):
        same = jnp.where(seg_row(distance) == lead, 1.0, 0.0)
        earlier = earlier + jnp.sum(same, axis=1, keepdims=True)
    before = jnp.sum(jnp.where(mine < column, 1.0, 0.0), axis=1, keepdims=True)
    index = lax.broadcasted_iota(jnp.int32, (rows, 1), 0).astype(jnp.float32)
    positions = index - before + jnp.where(column == lead, earlier, 0.0)
    angles = positions * freq
    cosine = jnp.cos(angles)
    sine = jnp.sin(angles) * sign
    for kv in range(kv_heads):
        at = slice(kv * HD, (kv + 1) * HD)
        x = kraw[0, :, at].astype(jnp.float32)
        rot_ref[:, at] = (x * cosine + pltpu.roll(x, HALF, 1) * sine).astype(jnp.bfloat16)

    def far_phase(kv, carry):
        @pl.when(kv + 1 < kv_heads)
        def _():
            relay(has_eight, 8, (7, 8), kv + 1)

        relay(has_six, 6, (9,), kv)
        for half in range(2):
            arrive(me >= 5, 5, half, kv)
            arrive(me >= 7, 7, half, kv)
        prepare(far_slots, kv)
        attend(far_slots, kv, False, True)
        return carry

    lax.fori_loop(0, kv_heads, far_phase, 0)

    for kind, (condition, source, distance, device) in flows.items():

        @pl.when(condition)
        def _():
            seg_copy(kind, source, distance, device).wait_send()

            def drain(kv, carry):
                for half in range(2):
                    piece_copy(kind, half, kv, source, distance, device).wait_send()
                return carry

            lax.fori_loop(0, kv_heads, drain, 0)


def local(queries, keys, values, segment_ids):
    rows = queries.shape[0]
    heads = queries.shape[1] // HD
    kv_heads = keys.shape[1] // HD
    count = lax.axis_size("seq")
    exponents = np.arange(HALF, dtype=np.float32) * np.float32(2.0 / HD)
    inverse = np.power(np.float32(ROPE_BASE), -exponents).astype(np.float32)
    frequencies = jnp.asarray(np.concatenate([inverse, inverse])[None])
    vmem = pl.BlockSpec(memory_space=pltpu.VMEM)
    hbm = pl.BlockSpec(memory_space=pltpu.HBM)
    flows = 11
    return pl.pallas_call(
        partial(kernel, kv_heads, count),
        out_shape=(
            pltpu.VMEM(queries.shape, jnp.bfloat16),
            pltpu.VMEM(keys.shape, jnp.bfloat16),
        ),
        in_specs=[hbm] * 4 + [vmem],
        out_specs=(vmem, vmem),
        scratch_shapes=[
            pltpu.VMEM((SLOTS, rows, kv_heads * HD), jnp.bfloat16),
            pltpu.VMEM((SLOTS, rows, kv_heads * HD), jnp.bfloat16),
            pltpu.VMEM((SLOTS, 1, rows), jnp.int32),
            pltpu.VMEM(queries.shape, jnp.bfloat16),
            pltpu.VMEM((heads, rows, HD), jnp.bfloat16),
            pltpu.VMEM((rows, HD), jnp.bfloat16),
            pltpu.VMEM((kv_heads, SPAN + 1, rows, HD), jnp.bfloat16),
            pltpu.VMEM((SPAN + 1, rows, HD), jnp.bfloat16),
            pltpu.VMEM((kv_heads, HD + ONES_ROWS, (SPAN + 1) * rows), jnp.bfloat16),
            pltpu.VMEM((SPAN + 1, rows, HD), jnp.float32),
            pltpu.VMEM((SPAN + 1, rows, HD), jnp.float32),
            pltpu.VMEM((rows, rows), jnp.float32),
            pltpu.VMEM((4 * rows, rows), jnp.float32),
            pltpu.VMEM((4 * rows, rows), jnp.float32),
            pltpu.VMEM((heads, 1, rows), jnp.float32),
            pltpu.VMEM((heads, HD + ONES_ROWS, rows), jnp.float32),
            pltpu.SemaphoreType.DMA((1 + 3 * kv_heads,)),
            pltpu.SemaphoreType.DMA((flows, kv_heads, 2)),
            pltpu.SemaphoreType.DMA((SLOTS, kv_heads, 2)),
            pltpu.SemaphoreType.DMA((flows,)),
            pltpu.SemaphoreType.DMA((SLOTS,)),
        ],
        compiler_params=pltpu.CompilerParams(
            vmem_limit_bytes=44 * 1024 * 1024, collective_id=0, has_side_effects=True
        ),
    )(queries, keys, values, segment_ids.reshape(1, rows), frequencies)


def solution(mesh):
    in_specs = (
        P(("groups", "seq"), None),
        P(("groups", "seq"), None),
        P(("groups", "seq"), None),
        P(("groups", "seq")),
    )
    out_specs = (P(("groups", "seq"), None), P(("groups", "seq"), None))
    return jax.shard_map(local, mesh=mesh, in_specs=in_specs, out_specs=out_specs, check_vma=False)
```

time: 84.3 us -> 53.9 us (0.64); the launches traced: 82.9 us -> 53.7 us
  Pallas kernels: 73.3 us -> 46.2 us
  other arithmetic: 2.59 us -> 0 us
    pallas_call x1, Pallas kernels: 73.3 us -> 46.2 us  [local(): pl.pallas_call(partial(kernel, kv_heads, count), out_shape=(pltpu.VMEM(qu...]
    unnamed x13 -> x12, local copies, waits for them, and re-layouts: 4.69 us -> 6.84 us
    slice x3 -> x0, local copies, waits for them, and re-layouts: 1.34 us -> none  [the longest x2 1.01 us: local(): pieces.append(jnp.concatenate([turned[:, part], values[:, part]], axis=1))]
where the time goes in v1:
time: 53.9 us; the launch traced here: 53.7 us
  Pallas kernels  46.2 us (86%)
  local copies, waits for them, and re-layouts  6.84 us (13%)
  between operations  0.65 us (1%)
    pallas_call x1, Pallas kernels, local(): pl.pallas_call(partial(kernel, kv_heads, count), out_shape=(pltpu.VMEM(qu...  46.2 us
    unnamed x12, local copies, waits for them, and re-layouts  6.84 us

profile of v1, /device:TPU:17, one launch (start us, length us, event | category | flops | bytes accessed | tf_op | source)
XLA Modules:
  0.0 53.7 jit_solution(9912354887277523890)
XLA Ops:
  0.6 0.0 copy-start
  0.6 1.6 %copy-done = bf16[256,4096]{1,0:T(8,128)(2,1)S(1)} copy-done((bf16[256,4096]{1,0:T(8,128)(2,1)S(1)}, bf16[256,4096]{1,0:T(8,128)(2,1)}, u32[]{:S(2)}) %copy-start) | copy-done | bytes 2097176
  2.2 0.0 copy-start.1
  2.2 0.9 %copy-done.1 = bf16[256,512]{1,0:T(8,128)(2,1)S(1)} copy-done((bf16[256,512]{1,0:T(8,128)(2,1)S(1)}, bf16[256,512]{1,0:T(8,128)(2,1)}, u32[]{:S(2)}) %copy-start.1) | copy-done | bytes 262168
  3.2 0.0 copy-start.2
  3.2 0.9 %copy-done.2 = bf16[256,512]{1,0:T(8,128)(2,1)S(1)} copy-done((bf16[256,512]{1,0:T(8,128)(2,1)S(1)}, bf16[256,512]{1,0:T(8,128)(2,1)}, u32[]{:S(2)}) %copy-start.2) | copy-done | bytes 262168
  4.1 0.0 copy-start.3
  4.1 0.7 %copy-done.3 = s32[256]{0:T(256)S(1)} copy-done((s32[256]{0:T(256)S(1)}, s32[256]{0:T(256)}, u32[]{:S(2)}) %copy-start.3) | copy-done | bytes 1048
  4.8 0.0 copy-start.4
  4.8 0.7 %copy-done.4 = f32[1,128]{1,0:T(1,128)S(1)} copy-done((f32[1,128]{1,0:T(1,128)S(1)}, f32[1,128]{1,0:T(1,128)}, u32[]{:S(2)}) %copy-start.4) | copy-done | bytes 536
  5.5 46.2 %shard_map.68 = (bf16[256,4096]{1,0:T(8,128)(2,1)S(1)}, bf16[256,512]{1,0:T(8,128)(2,1)S(1)}) custom-call(bf16[256,4096]{1,0:T(8,128)(2,1)S(1)} %copy-done, bf16[256,512]{1,0:T(8,128)(2,1)S(1)} %copy-done.1, bf16[256,512]{1,0:T(8,128)(2,1)S(1)} %copy-done.2, s32[1,256]{1,0:T(1,128)S(1)} %bitcast.1, f32[1,128]{1,0:T(1,128)S(1)} %copy-done.4), custom_call_target="tpu_custom_call" | custom-call | tf_op jit(solution)/shard_map/pallas_call | solution.py:400
  51.6 1.3 %copy.9 = bf16[256,4096]{1,0:T(8,128)(2,1)} copy(bf16[256,4096]{1,0:T(8,128)(2,1)S(1)} %get-tuple-element.2) | data formatting | bytes 4194304
  53.0 0.7 %copy.10 = bf16[256,512]{1,0:T(8,128)(2,1)} copy(bf16[256,512]{1,0:T(8,128)(2,1)S(1)} %get-tuple-element.3) | data formatting | bytes 524288
Async XLA Ops:
  0.6 1.6 %copy-start = (bf16[256,4096]{1,0:T(8,128)(2,1)S(1)}, bf16[256,4096]{1,0:T(8,128)(2,1)}, u32[]{:S(2)}) copy-start(bf16[256,4096]{1,0:T(8,128)(2,1)} %q_hbm.1) | copy-start | bytes 6291460
  2.2 0.9 %copy-start.1 = (bf16[256,512]{1,0:T(8,128)(2,1)S(1)}, bf16[256,512]{1,0:T(8,128)(2,1)}, u32[]{:S(2)}) copy-start(bf16[256,512]{1,0:T(8,128)(2,1)} %k_hbm.1) | copy-start | bytes 786436
  3.2 0.9 %copy-start.2 = (bf16[256,512]{1,0:T(8,128)(2,1)S(1)}, bf16[256,512]{1,0:T(8,128)(2,1)}, u32[]{:S(2)}) copy-start(bf16[256,512]{1,0:T(8,128)(2,1)} %v_hbm.1) | copy-start | bytes 786436
  4.1 0.7 %copy-start.3 = (s32[256]{0:T(256)S(1)}, s32[256]{0:T(256)}, u32[]{:S(2)}) copy-start(s32[256]{0:T(256)} %param.8) | copy-start | bytes 3076
  4.8 0.7 %copy-start.4 = (f32[1,128]{1,0:T(1,128)S(1)}, f32[1,128]{1,0:T(1,128)}, u32[]{:S(2)}) copy-start(f32[1,128]{1,0:T(1,128)} %constant.2.clone.freq_ref) | copy-start | bytes 1540

commit v2 on v1

--- a/solution.py
+++ b/solution.py
@@ -22,8 +22,9 @@
 
 def kernel(
     kv_heads, count, q_hbm, k_hbm, v_hbm, seg_hbm, freq_ref, out_ref, rot_ref,
-    kraw, vraw, segs, qraw, qa, qext, krot, kext, vt, ctab, stab, mask, scores_a, scores_b,
-    top, acc, local_sems, send_sems, recv_sems, seg_send, seg_recv,
+    kraw, vraw, segs, qraw, qa, qext, krot, kext, vt_a, vt_b, ctab, stab, mask,
+    scores_a, scores_b, weights_a, weights_b, top, fade, acc,
+    local_sems, send_sems, recv_sems, seg_send, seg_recv,
 ):
     rows = kraw.shape[1]
     heads = qa.shape[0]
@@ -210,10 +211,14 @@
     for one in q_loads:
         one.wait()
 
+    turn_c = (ctab[0] * scale).T[:HALF]
+    turn_s = (base_s * scale).T[:HALF]
+
     def turn(head, carry):
-        x = qraw[:, columns(head)].astype(jnp.float32)
-        turned = x * (ctab[0] * scale) + pltpu.roll(x, HALF, 1) * (stab[0] * scale)
-        qa[head] = turned.astype(jnp.bfloat16)
+        x = qraw[:, columns(head)].astype(jnp.float32).T
+        low, high = x[:HALF], x[HALF:]
+        qa[head, :HALF, :] = (low * turn_c - high * turn_s).astype(jnp.bfloat16)
+        qa[head, HALF:, :] = (high * turn_c + low * turn_s).astype(jnp.bfloat16)
         return carry
 
     lax.fori_loop(0, heads, turn, 0, unroll=4)
@@ -226,15 +231,15 @@
     row_at = lax.broadcasted_iota(jnp.int32, (HD, rows), 0)
     lane_at = lax.broadcasted_iota(jnp.int32, (rows, HD), 1)
     column = jnp.broadcast_to(mine, (HD, rows)).T[:, :1]
-    barred = jnp.where(column == lead, 0.0, -BIG)
-    ones_lane = jnp.where((lane_at >= 1) & (lane_at <= SPAN), 1.0, 0.0)
-    qext[...] = jnp.where(lane_at == 0, barred, ones_lane).astype(jnp.bfloat16)
+    barred = jnp.where(mine == lead, 0.0, -BIG)
+    ones_row = jnp.where((row_at >= 1) & (row_at <= SPAN), 1.0, 0.0)
+    qext[...] = jnp.where(row_at == 0, barred, ones_row).astype(jnp.bfloat16)
     key_at = lax.broadcasted_iota(jnp.int32, (rows, rows), 0)
     query_at = lax.broadcasted_iota(jnp.int32, (rows, rows), 1)
     mask[...] = jnp.where((key_at <= query_at) & (column == mine), 0.0, -BIG)
 
-    for kv in range(kv_heads):
-        vt[kv, HD:, :] = jnp.ones((ONES_ROWS, vt.shape[2]), jnp.bfloat16)
+    for vt in (vt_a, vt_b):
+        vt[:, HD:, :] = jnp.ones((vt.shape[0], ONES_ROWS, rows), jnp.bfloat16)
 
     def key_masks(slots):
         flat = jnp.where(row_at == 0, 1.0, 0.0)
@@ -246,100 +251,190 @@
             keep = (lane_at == 0) | (lane_at == slot)
             kext[slot] = jnp.where(keep, turned, 0.0).astype(jnp.bfloat16)
 
-    def prepare(slots, kv):
-        for slot in slots:
+    scores, weights, flipped = (scores_a, scores_b), (weights_a, weights_b), (vt_a, vt_b)
+    group_at = range(group)
+
+    def turn_keys(unit):
+        slots, kv, _, _ = unit
+        for i, slot in enumerate(slots):
             x = kraw[slot, :, columns(kv)].astype(jnp.float32)
             turned = x * ctab[slot] + pltpu.roll(x, HALF, 1) * stab[slot]
-            krot[kv, slot] = turned.astype(jnp.bfloat16)
-            flipped = vraw[slot, :, columns(kv)].astype(jnp.float32).T
-            vt[kv, :HD, slot * rows : (slot + 1) * rows] = flipped.astype(jnp.bfloat16)
-
-    def attend(slots, kv, first, last):
-        tops = {}
-
-        def score(head, buffer):
-            query = qa[head]
-            if not first:
-                query = jnp.concatenate([query, qext[...]], axis=1)
+            krot[i] = turned.astype(jnp.bfloat16)
+
+    def flip_values(unit, vt):
+        slots, kv, _, _ = unit
+        for i, slot in enumerate(slots):
+            turned = vraw[slot, :, columns(kv)].astype(jnp.float32).T
+            vt[i, :HD, :] = turned.astype(jnp.bfloat16)
+
+    def score(unit, buffer):
+        slots, kv, first, _ = unit
+        for t in group_at:
+            head = kv * group + t
             best = None
             for i, slot in enumerate(slots):
-                key = krot[kv, slot]
+                key, query = krot[i], qa[head]
                 if not first:
                     key = jnp.concatenate([key, kext[slot]], axis=1)
-                part = lax.dot_general(
-                    key, query, (((1,), (1,)), ((), ())), preferred_element_type=jnp.float32
-                )
+                    query = jnp.concatenate([query, qext[...]], axis=0)
+                part = jnp.dot(key, query, preferred_element_type=jnp.float32)
                 if first:
                     part = part + mask[...]
-                buffer[i * rows : (i + 1) * rows, :] = part
+                buffer[t, i * rows : (i + 1) * rows, :] = part
                 high = jnp.max(part.reshape(rows // 8, 8, rows), axis=0)
                 best = high if best is None else jnp.maximum(best, high)
-            return jnp.max(best, axis=0, keepdims=True)
-
-        def weigh(head, buffer, new_top):
-            if not first:
-                old_top = top[head]
-                new_top = jnp.maximum(new_top, old_top)
+                if i + 1 == len(slots):
+                    new_top = jnp.max(best, axis=0, keepdims=True)
+                    if not first:
+                        old_top = top[head]
+                        new_top = jnp.maximum(old_top, new_top)
+                        fade[head] = jnp.exp2(old_top - new_top)
+                    top[head] = new_top
+                yield
+
+    def weigh(unit, source, target):
+        slots, kv, _, _ = unit
+        for t in group_at:
+            height = top[kv * group + t]
+            for i in range(len(slots)):
+                at = slice(i * rows, (i + 1) * rows)
+                target[t, at, :] = jnp.exp2(source[t, at, :] - height).astype(jnp.bfloat16)
+                yield
+
+    def mix(unit, source, vt):
+        slots, kv, first, last = unit
+        for t in group_at:
+            head = kv * group + t
             mixed = None
-            for i, slot in enumerate(slots):
-                part = buffer[i * rows : (i + 1) * rows, :]
-                weights = jnp.exp2(part - new_top).astype(jnp.bfloat16)
-                at = slice(slot * rows, (slot + 1) * rows)
-                term = jnp.dot(vt[kv, :, at], weights, preferred_element_type=jnp.float32)
+            for i in range(len(slots)):
+                part = source[t, i * rows : (i + 1) * rows, :]
+                term = jnp.dot(vt[i], part, preferred_element_type=jnp.float32)
                 mixed = term if mixed is None else mixed + term
-            if not first:
-                mixed = mixed + acc[head] * jnp.exp2(old_top - new_top)
-            if last:
-                result = mixed[:HD] * (1.0 / mixed[HD : HD + 1])
-                out_ref[:, columns(head)] = result.T.astype(jnp.bfloat16)
-            else:
-                top[head] = new_top
-                acc[head] = mixed
-
-        buffers = (scores_a, scores_b)
-        tops[0] = score(kv * group, buffers[0])
-        for i in range(group):
-            if i + 1 < group:
-                tops[i + 1] = score(kv * group + i + 1, buffers[(i + 1) % 2])
-            weigh(kv * group + i, buffers[i % 2], tops[i])
-
-    near_slots = (1, 2, 3, 4)
-    far_slots = (5, 6, 7)
-
-    def own_phase(kv, carry):
-        prepare((0,), kv)
-        attend((0,), kv, True, False)
+                if i + 1 == len(slots):
+                    if not first:
+                        mixed = mixed + acc[head] * fade[head]
+                    if last:
+                        result = mixed[:HD] * (1.0 / mixed[HD : HD + 1])
+                        out_ref[:, columns(head)] = result.T.astype(jnp.bfloat16)
+                    else:
+                        acc[head] = mixed
+                yield
+
+    def step(parity, newest, middle, oldest):
+        streams = []
+        if newest is not None:
+            turn_keys(newest)
+            streams.append((score(newest, scores[parity]), len(newest[0])))
+        if middle is not None:
+            flip_values(middle, flipped[1 - parity])
+            streams.append((weigh(middle, scores[1 - parity], weights[1 - parity]), len(middle[0])))
+        if oldest is not None:
+            streams.append((mix(oldest, weights[parity], flipped[parity]), len(oldest[0])))
+        beats = [
+            ((k + 0.5) / (group * n), place, stream)
+            for place, (stream, n) in enumerate(streams)
+            for k in range(group * n)
+        ]
+        for _, _, stream in sorted(beats, key=lambda beat: beat[:2]):
+            next(stream)
+
+    far_slots = (5 - 4 * core, 6, 7)
+
+    def own(kv):
+        return ((0,), kv, True, False)
+
+    def pair(index):
+        base = 3 + core - 2 * (index // kv_heads)
+        return ((base, base + 1), index % kv_heads, False, False)
+
+    def rest(kv):
+        return (far_slots, kv, False, True)
+
+    def get_four(kv):
+        relay(has_behind, 4, (3, 4, 5), kv)
+
+    def get_two(kv):
+        relay(has_two, 2, (6, 10), kv)
+
+    def get_eight(kv):
+        relay(has_eight, 8, (7, 8), kv)
+
+    def get_six(kv):
+        relay(has_six, 6, (9,), kv)
+
+    def get_beside(condition, distance, kv):
+        for half in range(2):
+            arrive(condition, distance, half, kv)
+
+    def get_beside_four(kv):
+        get_beside(has_behind, 3 + 2 * core, kv)
+
+    def get_beside_two(kv):
+        get_beside(has_two, 1 + 2 * core, kv)
+
+    def get_far(kv):
+        get_beside(has_six, 5 + 2 * core, kv)
+        get_beside((plane >= 2) & (core == 0), 7, kv)
+        get_beside(core == 1, 1, kv)
+
+    step(0, own(0), None, None)
+    step(1, own(1), own(0), None)
+    step(0, own(2), own(1), own(0))
+    step(1, own(3), own(2), own(1))
+
+    relay_segs(has_behind, 4, (3, 4, 5))
+    get_four(0)
+    arrive_segs(has_behind, 3 + 2 * core)
+    key_masks((3 + core, 4 + core))
+    get_beside_four(0)
+    step(0, pair(0), own(3), own(2))
+    get_four(1)
+    get_beside_four(1)
+    step(1, pair(1), pair(0), own(3))
+
+    relay_segs(has_two, 2, (6, 10))
+    arrive_segs(has_two, 1 + 2 * core)
+    key_masks((1 + core, 2 + core))
+
+    def ready(index):
+        @pl.when(index < kv_heads)
+        def _():
+            get_four(index)
+
+        @pl.when(index < kv_heads + 2)
+        def _():
+            get_two(index - 2)
+
+        @pl.when(index < kv_heads)
+        def _():
+            get_beside_four(index)
+
+        @pl.when(index >= kv_heads)
+        def _():
+            get_beside_two(index - kv_heads)
+
+        @pl.when(index >= kv_heads + 2)
+        def _():
+            get_eight(index - kv_heads - 2)
+
+    def pairs(turn, carry):
+        index = 2 * turn + 2
+        ready(index)
+        step(0, pair(index), pair(index - 1), pair(index - 2))
+        ready(index + 1)
+        step(1, pair(index + 1), pair(index), pair(index - 1))
         return carry
 
-    lax.fori_loop(0, kv_heads, own_phase, 0)
-
-    relay_segs(has_behind, 4, (3, 4, 5))
-    relay(has_behind, 4, (3, 4, 5), 0)
-    relay_segs(has_two, 2, (6, 10))
-    arrive_segs(me >= 1, 1)
-    arrive_segs(me >= 3, 3)
-    key_masks(near_slots)
-
-    def near_phase(kv, carry):
-        @pl.when(kv + 1 < kv_heads)
-        def _():
-            relay(has_behind, 4, (3, 4, 5), kv + 1)
-
-        relay(has_two, 2, (6, 10), kv)
-        for half in range(2):
-            arrive(me >= 1, 1, half, kv)
-            arrive(me >= 3, 3, half, kv)
-        prepare(near_slots, kv)
-        attend(near_slots, kv, False, False)
-        return carry
-
-    lax.fori_loop(0, kv_heads, near_phase, 0)
+    lax.fori_loop(0, kv_heads - 1, pairs, 0)
+    final = 2 * kv_heads
 
     relay_segs(has_eight, 8, (7, 8))
-    relay(has_eight, 8, (7, 8), 0)
+    get_eight(2)
     relay_segs(has_six, 6, (9,))
-    arrive_segs(me >= 5, 5)
-    arrive_segs(me >= 7, 7)
+    get_six(0)
+    arrive_segs(has_six, 5 + 2 * core)
+    arrive_segs((plane >= 2) & (core == 0), 7)
+    arrive_segs(core == 1, 1)
     key_masks(far_slots)
 
     earlier = jnp.zeros((1, 1), jnp.float32)
@@ -357,20 +452,20 @@
         x = kraw[0, :, at].astype(jnp.float32)
         rot_ref[:, at] = (x * cosine + pltpu.roll(x, HALF, 1) * sine).astype(jnp.bfloat16)
 
-    def far_phase(kv, carry):
-        @pl.when(kv + 1 < kv_heads)
-        def _():
-            relay(has_eight, 8, (7, 8), kv + 1)
-
-        relay(has_six, 6, (9,), kv)
-        for half in range(2):
-            arrive(me >= 5, 5, half, kv)
-            arrive(me >= 7, 7, half, kv)
-        prepare(far_slots, kv)
-        attend(far_slots, kv, False, True)
-        return carry
-
-    lax.fori_loop(0, kv_heads, far_phase, 0)
+    get_far(0)
+    get_six(1)
+    step(0, rest(0), pair(final - 1), pair(final - 2))
+    get_eight(3)
+    get_far(1)
+    get_six(2)
+    step(1, rest(1), rest(0), pair(final - 1))
+    get_far(2)
+    get_six(3)
+    step(0, rest(2), rest(1), rest(0))
+    get_far(3)
+    step(1, rest(3), rest(2), rest(1))
+    step(0, None, rest(3), rest(2))
+    step(1, None, None, rest(3))
 
     for kind, (condition, source, distance, device) in flows.items():
 
@@ -410,16 +505,20 @@
             pltpu.VMEM((SLOTS, rows, kv_heads * HD), jnp.bfloat16),
             pltpu.VMEM((SLOTS, 1, rows), jnp.int32),
             pltpu.VMEM(queries.shape, jnp.bfloat16),
-            pltpu.VMEM((heads, rows, HD), jnp.bfloat16),
-            pltpu.VMEM((rows, HD), jnp.bfloat16),
-            pltpu.VMEM((kv_heads, SPAN + 1, rows, HD), jnp.bfloat16),
+            pltpu.VMEM((heads, HD, rows), jnp.bfloat16),
+            pltpu.VMEM((HD, rows), jnp.bfloat16),
+            pltpu.VMEM((3, rows, HD), jnp.bfloat16),
             pltpu.VMEM((SPAN + 1, rows, HD), jnp.bfloat16),
-            pltpu.VMEM((kv_heads, HD + ONES_ROWS, (SPAN + 1) * rows), jnp.bfloat16),
+            pltpu.VMEM((3, HD + ONES_ROWS, rows), jnp.bfloat16),
+            pltpu.VMEM((3, HD + ONES_ROWS, rows), jnp.bfloat16),
             pltpu.VMEM((SPAN + 1, rows, HD), jnp.float32),
             pltpu.VMEM((SPAN + 1, rows, HD), jnp.float32),
             pltpu.VMEM((rows, rows), jnp.float32),
-            pltpu.VMEM((4 * rows, rows), jnp.float32),
-            pltpu.VMEM((4 * rows, rows), jnp.float32),
+            pltpu.VMEM((heads // kv_heads, 3 * rows, rows), jnp.float32),
+            pltpu.VMEM((heads // kv_heads, 3 * rows, rows), jnp.float32),
+            pltpu.VMEM((heads // kv_heads, 3 * rows, rows), jnp.bfloat16),
+            pltpu.VMEM((heads // kv_heads, 3 * rows, rows), jnp.bfloat16),
+            pltpu.VMEM((heads, 1, rows), jnp.float32),
             pltpu.VMEM((heads, 1, rows), jnp.float32),
             pltpu.VMEM((heads, HD + ONES_ROWS, rows), jnp.float32),
             pltpu.SemaphoreType.DMA((1 + 3 * kv_heads,)),
@@ -429,9 +528,15 @@
             pltpu.SemaphoreType.DMA((SLOTS,)),
         ],
         compiler_params=pltpu.CompilerParams(
-            vmem_limit_bytes=44 * 1024 * 1024, collective_id=0, has_side_effects=True
+            vmem_limit_bytes=56 * 1024 * 1024, collective_id=0, has_side_effects=True
         ),
-    )(queries, keys, values, segment_ids.reshape(1, rows), frequencies)
+    )(
+        *[
+            pltpu.with_memory_space_constraint(x, pltpu.HBM)
+            for x in (queries, keys, values, segment_ids.reshape(1, rows))
+        ],
+        frequencies,
+    )
 
 
 def solution(mesh):

time: 53.9 us -> 42.3 us (0.78)
  Pallas kernels: 46.2 us -> 39.4 us
  local copies, waits for them, and re-layouts: 6.84 us -> 2.02 us
    pallas_call x1, Pallas kernels: 46.2 us -> 39.4 us  [local(): pl.pallas_call(partial(kernel, kv_heads, count), out_shape=(pltpu.VMEM(qu...]
    unnamed x12 -> x2, local copies, waits for them, and re-layouts: 6.84 us -> 2.02 us
where the time goes in v2:
time: 42.3 us; the launch traced here: 42.1 us
  Pallas kernels  39.4 us (93%)
  local copies, waits for them, and re-layouts  2.02 us (5%)
  between operations  0.64 us (2%)
    pallas_call x1, Pallas kernels, local(): pl.pallas_call(partial(kernel, kv_heads, count), out_shape=(pltpu.VMEM(qu...  39.4 us
    unnamed x2, local copies, waits for them, and re-layouts  2.02 us

profile of v2, /device:TPU:17, one launch (start us, length us, event | category | flops | bytes accessed | tf_op | source)
XLA Modules:
  0.0 42.1 jit_solution(5090724026413867496)
XLA Ops:
  0.6 39.4 %shard_map.68 = (bf16[256,4096]{1,0:T(8,128)(2,1)S(1)}, bf16[256,512]{1,0:T(8,128)(2,1)S(1)}) custom-call(bf16[256,4096]{1,0:T(8,128)(2,1)} %q_hbm.1, bf16[256,512]{1,0:T(8,128)(2,1)} %k_hbm.1, bf16[256,512]{1,0:T(8,128)(2,1)} %v_hbm.1, s32[1,256]{1,0:T(1,128)} %bitcast.1, f32[1,128]{1,0:T(1,128)} %constant.2.clone.freq_ref), custom_call_target="tpu_custom_call" | custom-call | tf_op jit(solution)/shard_map/pallas_call | solution.py:495
  40.1 1.3 %copy.9 = bf16[256,4096]{1,0:T(8,128)(2,1)} copy(bf16[256,4096]{1,0:T(8,128)(2,1)S(1)} %get-tuple-element.2) | data formatting | bytes 4194304
  41.4 0.7 %copy.10 = bf16[256,512]{1,0:T(8,128)(2,1)} copy(bf16[256,512]{1,0:T(8,128)(2,1)S(1)} %get-tuple-element.3) | data formatting | bytes 524288

commit v3 on v2

--- a/solution.py
+++ b/solution.py
@@ -2,7 +2,6 @@
 
 import jax
 import jax.numpy as jnp
-import numpy as np
 from jax import lax
 from jax.experimental import pallas as pl
 from jax.experimental.pallas import tpu as pltpu
@@ -11,22 +10,22 @@
 HD = 128
 HALF = HD // 2
 SPAN = 7
-ROPE_BASE = 1000000.0
 BIG = 1e30
 NO_SEGMENT = -1
 ONES_ROWS = 16
 STEP = 16
 SLOTS = SPAN + 2
 LOG2E = 1.4426950408889634
+LOG2_BASE = 19.931568569324174
 
 
 def kernel(
-    kv_heads, count, q_hbm, k_hbm, v_hbm, seg_hbm, freq_ref, out_ref, rot_ref,
+    kv_heads, count, q_hbm, k_hbm, v_hbm, seg_hbm, out_ref, rot_ref,
     kraw, vraw, segs, qraw, qa, qext, krot, kext, vt_a, vt_b, ctab, stab, mask,
     scores_a, scores_b, weights_a, weights_b, top, fade, acc,
     local_sems, send_sems, recv_sems, seg_send, seg_recv,
 ):
-    rows = kraw.shape[1]
+    rows = kraw.shape[2]
     heads = qa.shape[0]
     group = heads // kv_heads
     me = lax.axis_index("seq")
@@ -37,7 +36,6 @@
     partner = me + 1 - 2 * core
     across = me + 2 - 4 * side
     ahead = me + 4
-    behind = me - 4
     has_ahead = plane + 1 < planes
     has_behind = plane >= 1
 
@@ -48,16 +46,15 @@
             barrier, inc=1, device_id={"seq": device}, device_id_type=pl.DeviceIdType.MESH
         )
 
-    greet(partner)
-    greet(across)
-
-    @pl.when(has_ahead)
-    def _():
-        greet(ahead)
-
-    @pl.when(has_behind)
-    def _():
-        greet(behind)
+    for distance in range(1, SPAN + 1):
+
+        @pl.when(me >= distance)
+        def _():
+            greet(me - distance)
+
+        @pl.when(me + distance < count)
+        def _():
+            greet(me + distance)
 
     def columns(kv):
         return pl.ds(pl.multiple_of(kv * HD, HD), HD)
@@ -71,8 +68,8 @@
     for kv in range(kv_heads):
         at = slice(kv * HD, (kv + 1) * HD)
         loads.append((
-            load(1 + 2 * kv, k_hbm.at[:, at], kraw.at[0, :, at]),
-            load(2 + 2 * kv, v_hbm.at[:, at], vraw.at[0, :, at]),
+            load(1 + 2 * kv, k_hbm.at[:, at], kraw.at[0, kv]),
+            load(2 + 2 * kv, v_hbm.at[:, at], vraw.at[0, kv]),
         ))
         for one in loads[-1]:
             one.start()
@@ -83,33 +80,28 @@
         q_loads.append(load(1 + 2 * kv_heads + kv, q_hbm.at[:, at], qraw.at[:, at]))
         q_loads[-1].start()
 
-    both = has_ahead & has_behind
-    one_side = (has_ahead | has_behind) & jnp.logical_not(both)
-    neither = jnp.logical_not(has_ahead | has_behind)
-    for extra, condition in ((2, both), (1, one_side), (0, neither)):
-
-        @pl.when(condition)
-        def _():
-            pl.semaphore_wait(barrier, 2 + extra)
+    before_me = jnp.minimum(me, SPAN)
+    after_me = jnp.minimum(count - 1 - me, SPAN)
+    pl.semaphore_wait(barrier, before_me + after_me)
 
     def piece_copy(kind, half, kv, source, distance, device):
         buffer = (kraw, vraw)[half]
         return pltpu.make_async_remote_copy(
-            src_ref=buffer.at[source, :, columns(kv)],
-            dst_ref=buffer.at[distance, :, columns(kv)],
+            src_ref=buffer.at[source, kv],
+            dst_ref=buffer.at[distance, kv],
             send_sem=send_sems.at[kind, kv, half],
             recv_sem=recv_sems.at[distance, kv, half],
             device_id={"seq": device},
             device_id_type=pl.DeviceIdType.MESH,
         )
 
-    def seg_copy(kind, source, distance, device):
+    def seg_copy(distance):
         return pltpu.make_async_remote_copy(
-            src_ref=segs.at[source],
+            src_ref=segs.at[0],
             dst_ref=segs.at[distance],
-            send_sem=seg_send.at[kind],
+            send_sem=seg_send.at[distance],
             recv_sem=seg_recv.at[distance],
-            device_id={"seq": device},
+            device_id={"seq": me + distance},
             device_id_type=pl.DeviceIdType.MESH,
         )
 
@@ -130,45 +122,46 @@
         8: (has_eight, 8, 7, partner),
         9: (has_six, 6, 6 + to_partner, partner),
         10: ((side == 0) & (core == 0) & has_behind & has_ahead, 2, 6, ahead),
+        11: ((side == 1) & has_ahead, 2, 6, ahead),
     }
 
-    def send(kinds, half, kv):
+    def carries(kind, kv):
+        condition = flows[kind][0]
+        final = kv == kv_heads - 1
+        if kind == 3 and final:
+            return condition & (side == 1)
+        if kind == 11 and not final:
+            return None
+        return condition
+
+    def send(kinds, half, kv, allowed=True):
         for kind in kinds:
-            condition, source, distance, device = flows[kind]
-
-            @pl.when(condition)
+            _, source, distance, device = flows[kind]
+            condition = carries(kind, kv)
+            if condition is None:
+                continue
+
+            @pl.when(condition & allowed)
             def _():
                 piece_copy(kind, half, kv, source, distance, device).start()
 
-    def send_segs(kinds):
-        for kind in kinds:
-            condition, source, distance, device = flows[kind]
-
-            @pl.when(condition)
-            def _():
-                seg_copy(kind, source, distance, device).start()
-
     def arrive(condition, distance, half, kv):
         @pl.when(condition)
         def _():
             piece_copy(0, half, kv, 0, distance, partner).wait_recv()
 
-    def arrive_segs(condition, distance):
-        @pl.when(condition)
-        def _():
-            seg_copy(0, 0, distance, partner).wait_recv()
-
-    def relay(condition, distance, kinds, kv):
-        for half in range(2):
+    def relay(condition, distance, kinds, kv, halves=(0, 1)):
+        for half in halves:
             arrive(condition, distance, half, kv)
-            send(kinds, half, kv)
-
-    def relay_segs(condition, distance, kinds):
-        arrive_segs(condition, distance)
-        send_segs(kinds)
+            send(kinds, half, kv, condition)
 
     seg_load.wait()
-    send_segs((0, 1, 2))
+    for distance in range(1, SPAN + 1):
+
+        @pl.when(me + distance < count)
+        def _():
+            seg_copy(distance).start()
+
     for kv in range(kv_heads):
         for half in range(2):
             loads[kv][half].wait()
@@ -182,8 +175,9 @@
             kraw[distance] = jnp.zeros(kraw.shape[1:], jnp.bfloat16)
             vraw[distance] = jnp.zeros(vraw.shape[1:], jnp.bfloat16)
 
-    freq = freq_ref[...]
     lane = lax.broadcasted_iota(jnp.int32, (1, HD), 1)
+    pair_at = jnp.where(lane < HALF, lane, lane - HALF).astype(jnp.float32)
+    freq = jnp.exp2(pair_at * (-2.0 / HD * LOG2_BASE))
     sign = jnp.where(lane < HALF, -1.0, 1.0)
 
     def fan(steps, stride):
@@ -257,14 +251,14 @@
     def turn_keys(unit):
         slots, kv, _, _ = unit
         for i, slot in enumerate(slots):
-            x = kraw[slot, :, columns(kv)].astype(jnp.float32)
+            x = kraw[slot, kv].astype(jnp.float32)
             turned = x * ctab[slot] + pltpu.roll(x, HALF, 1) * stab[slot]
             krot[i] = turned.astype(jnp.bfloat16)
 
     def flip_values(unit, vt):
         slots, kv, _, _ = unit
         for i, slot in enumerate(slots):
-            turned = vraw[slot, :, columns(kv)].astype(jnp.float32).T
+            turned = vraw[slot, kv].astype(jnp.float32).T
             vt[i, :HD, :] = turned.astype(jnp.bfloat16)
 
     def score(unit, buffer):
@@ -320,19 +314,25 @@
                         acc[head] = mixed
                 yield
 
-    def step(parity, newest, middle, oldest):
+    def step(parity, newest, middle, oldest, closing=None):
         streams = []
         if newest is not None:
             turn_keys(newest)
-            streams.append((score(newest, scores[parity]), len(newest[0])))
+            streams.append((score(newest, scores[parity]), len(newest[0]), 0.0, 1.0))
         if middle is not None:
             flip_values(middle, flipped[1 - parity])
-            streams.append((weigh(middle, scores[1 - parity], weights[1 - parity]), len(middle[0])))
+            stream = weigh(middle, scores[1 - parity], weights[1 - parity])
+            streams.append((stream, len(middle[0]), 0.0, 1.0))
         if oldest is not None:
-            streams.append((mix(oldest, weights[parity], flipped[parity]), len(oldest[0])))
+            span = 1.0 if closing is None else 0.5
+            stream = mix(oldest, weights[parity], flipped[parity])
+            streams.append((stream, len(oldest[0]), 0.0, span))
+        if closing is not None:
+            stream = mix(closing, weights[1 - parity], flipped[1 - parity])
+            streams.append((stream, len(closing[0]), 0.55, 0.6))
         beats = [
-            ((k + 0.5) / (group * n), place, stream)
-            for place, (stream, n) in enumerate(streams)
+            (start + span * (k + 0.5) / (group * n), place, stream)
+            for place, (stream, n, start, span) in enumerate(streams)
             for k in range(group * n)
         ]
         for _, _, stream in sorted(beats, key=lambda beat: beat[:2]):
@@ -343,21 +343,23 @@
     def own(kv):
         return ((0,), kv, True, False)
 
-    def pair(index):
-        base = 3 + core - 2 * (index // kv_heads)
-        return ((base, base + 1), index % kv_heads, False, False)
+    def early(kv):
+        return ((3 + core, 4 + core), kv, False, False)
+
+    def later(kv):
+        return ((1 + core, 2 + core), kv, False, False)
 
     def rest(kv):
         return (far_slots, kv, False, True)
 
-    def get_four(kv):
-        relay(has_behind, 4, (3, 4, 5), kv)
+    def get_four(kv, halves=(0, 1)):
+        relay(has_behind, 4, (3, 4, 5), kv, halves)
 
     def get_two(kv):
-        relay(has_two, 2, (6, 10), kv)
-
-    def get_eight(kv):
-        relay(has_eight, 8, (7, 8), kv)
+        relay(has_two, 2, (6, 10, 11), kv)
+
+    def get_eight(kv, where):
+        relay(has_eight & (side == where), 8, (7, 8), kv)
 
     def get_six(kv):
         relay(has_six, 6, (9,), kv)
@@ -380,62 +382,19 @@
     step(0, own(0), None, None)
     step(1, own(1), own(0), None)
     step(0, own(2), own(1), own(0))
+    get_four(0, (0,))
     step(1, own(3), own(2), own(1))
-
-    relay_segs(has_behind, 4, (3, 4, 5))
-    get_four(0)
-    arrive_segs(has_behind, 3 + 2 * core)
-    key_masks((3 + core, 4 + core))
+    get_four(0, (1,))
+
+    for distance in range(1, SPAN + 1):
+
+        @pl.when(me >= distance)
+        def _():
+            seg_copy(distance).wait_recv()
+
+    key_masks(range(1, SPAN + 1))
     get_beside_four(0)
-    step(0, pair(0), own(3), own(2))
-    get_four(1)
-    get_beside_four(1)
-    step(1, pair(1), pair(0), own(3))
-
-    relay_segs(has_two, 2, (6, 10))
-    arrive_segs(has_two, 1 + 2 * core)
-    key_masks((1 + core, 2 + core))
-
-    def ready(index):
-        @pl.when(index < kv_heads)
-        def _():
-            get_four(index)
-
-        @pl.when(index < kv_heads + 2)
-        def _():
-            get_two(index - 2)
-
-        @pl.when(index < kv_heads)
-        def _():
-            get_beside_four(index)
-
-        @pl.when(index >= kv_heads)
-        def _():
-            get_beside_two(index - kv_heads)
-
-        @pl.when(index >= kv_heads + 2)
-        def _():
-            get_eight(index - kv_heads - 2)
-
-    def pairs(turn, carry):
-        index = 2 * turn + 2
-        ready(index)
-        step(0, pair(index), pair(index - 1), pair(index - 2))
-        ready(index + 1)
-        step(1, pair(index + 1), pair(index), pair(index - 1))
-        return carry
-
-    lax.fori_loop(0, kv_heads - 1, pairs, 0)
-    final = 2 * kv_heads
-
-    relay_segs(has_eight, 8, (7, 8))
-    get_eight(2)
-    relay_segs(has_six, 6, (9,))
-    get_six(0)
-    arrive_segs(has_six, 5 + 2 * core)
-    arrive_segs((plane >= 2) & (core == 0), 7)
-    arrive_segs(core == 1, 1)
-    key_masks(far_slots)
+    step(0, early(0), own(3), own(2))
 
     earlier = jnp.zeros((1, 1), jnp.float32)
     for distance in range(1, SPAN + 1):
@@ -449,36 +408,68 @@
     sine = jnp.sin(angles) * sign
     for kv in range(kv_heads):
         at = slice(kv * HD, (kv + 1) * HD)
-        x = kraw[0, :, at].astype(jnp.float32)
+        x = kraw[0, kv].astype(jnp.float32)
         rot_ref[:, at] = (x * cosine + pltpu.roll(x, HALF, 1) * sine).astype(jnp.bfloat16)
 
+    get_four(1)
+    get_beside_four(1)
+    step(1, early(1), early(0), own(3))
+    get_four(2)
+    get_two(0)
+    get_beside_four(2)
+    step(0, early(2), early(1), early(0))
+    get_beside_two(0)
+    step(1, later(0), early(2), early(1))
+    get_four(3)
+    get_two(1)
+    get_beside_four(3)
+    step(0, early(3), later(0), early(2))
+    get_beside_two(1)
+    get_eight(0, 1)
+    step(1, later(1), early(3), later(0))
+    get_two(2)
+    get_eight(0, 0)
+    get_eight(1, 1)
+    get_beside_two(2)
+    step(0, later(2), later(1), early(3))
+    get_two(3)
+    get_eight(1, 0)
+    get_eight(2, 1)
+    get_six(0)
+    get_beside_two(3)
+    step(1, later(3), later(2), later(1))
+    get_eight(3, 1)
+    get_six(1)
     get_far(0)
-    get_six(1)
-    step(0, rest(0), pair(final - 1), pair(final - 2))
-    get_eight(3)
+    step(0, rest(0), later(3), later(2))
+    get_eight(2, 0)
+    get_six(2)
     get_far(1)
-    get_six(2)
-    step(1, rest(1), rest(0), pair(final - 1))
+    step(1, rest(1), rest(0), later(3))
+    get_eight(3, 0)
+    get_six(3)
     get_far(2)
-    get_six(3)
     step(0, rest(2), rest(1), rest(0))
     get_far(3)
     step(1, rest(3), rest(2), rest(1))
-    step(0, None, rest(3), rest(2))
-    step(1, None, None, rest(3))
-
-    for kind, (condition, source, distance, device) in flows.items():
-
-        @pl.when(condition)
-        def _():
-            seg_copy(kind, source, distance, device).wait_send()
-
-            def drain(kv, carry):
+    step(0, None, rest(3), rest(2), rest(3))
+
+    for distance in range(1, SPAN + 1):
+
+        @pl.when(me + distance < count)
+        def _():
+            seg_copy(distance).wait_send()
+
+    for kind, (_, source, distance, device) in flows.items():
+        for kv in range(kv_heads):
+            condition = carries(kind, kv)
+            if condition is None:
+                continue
+
+            @pl.when(condition)
+            def _():
                 for half in range(2):
                     piece_copy(kind, half, kv, source, distance, device).wait_send()
-                return carry
-
-            lax.fori_loop(0, kv_heads, drain, 0)
 
 
 def local(queries, keys, values, segment_ids):
@@ -486,23 +477,20 @@
     heads = queries.shape[1] // HD
     kv_heads = keys.shape[1] // HD
     count = lax.axis_size("seq")
-    exponents = np.arange(HALF, dtype=np.float32) * np.float32(2.0 / HD)
-    inverse = np.power(np.float32(ROPE_BASE), -exponents).astype(np.float32)
-    frequencies = jnp.asarray(np.concatenate([inverse, inverse])[None])
     vmem = pl.BlockSpec(memory_space=pltpu.VMEM)
     hbm = pl.BlockSpec(memory_space=pltpu.HBM)
-    flows = 11
+    flows = 12
     return pl.pallas_call(
         partial(kernel, kv_heads, count),
         out_shape=(
             pltpu.VMEM(queries.shape, jnp.bfloat16),
             pltpu.VMEM(keys.shape, jnp.bfloat16),
         ),
-        in_specs=[hbm] * 4 + [vmem],
+        in_specs=[hbm] * 4,
         out_specs=(vmem, vmem),
         scratch_shapes=[
-            pltpu.VMEM((SLOTS, rows, kv_heads * HD), jnp.bfloat16),
-            pltpu.VMEM((SLOTS, rows, kv_heads * HD), jnp.bfloat16),
+            pltpu.VMEM((SLOTS, kv_heads, rows, HD), jnp.bfloat16),
+            pltpu.VMEM((SLOTS, kv_heads, rows, HD), jnp.bfloat16),
             pltpu.VMEM((SLOTS, 1, rows), jnp.int32),
             pltpu.VMEM(queries.shape, jnp.bfloat16),
             pltpu.VMEM((heads, HD, rows), jnp.bfloat16),
@@ -524,7 +512,7 @@
             pltpu.SemaphoreType.DMA((1 + 3 * kv_heads,)),
             pltpu.SemaphoreType.DMA((flows, kv_heads, 2)),
             pltpu.SemaphoreType.DMA((SLOTS, kv_heads, 2)),
-            pltpu.SemaphoreType.DMA((flows,)),
+            pltpu.SemaphoreType.DMA((SLOTS,)),
             pltpu.SemaphoreType.DMA((SLOTS,)),
         ],
         compiler_params=pltpu.CompilerParams(
@@ -535,7 +523,6 @@
             pltpu.with_memory_space_constraint(x, pltpu.HBM)
             for x in (queries, keys, values, segment_ids.reshape(1, rows))
         ],
-        frequencies,
     )
 
 

time: 42.3 us -> 41.3 us (0.976)
  Pallas kernels: 39.4 us -> 38.4 us
    pallas_call x1, Pallas kernels: 39.4 us -> 38.4 us  [local(): pl.pallas_call(partial(kernel, kv_heads, count), out_shape=(pltpu.VMEM(qu...]
where the time goes in v3:
time: 41.3 us; the launch traced here: 41 us
  Pallas kernels  38.4 us (93%)
  local copies, waits for them, and re-layouts  2.02 us (5%)
  between operations  0.64 us (2%)
    pallas_call x1, Pallas kernels, local(): pl.pallas_call(partial(kernel, kv_heads, count), out_shape=(pltpu.VMEM(qu...  38.4 us
    unnamed x2, local copies, waits for them, and re-layouts  2.02 us

profile of v3, /device:TPU:17, one launch (start us, length us, event | category | flops | bytes accessed | tf_op | source)
XLA Modules:
  0.0 41.0 jit_solution(13997839287009646370)
XLA Ops:
  0.6 38.4 %shard_map.59 = (bf16[256,4096]{1,0:T(8,128)(2,1)S(1)}, bf16[256,512]{1,0:T(8,128)(2,1)S(1)}) custom-call(bf16[256,4096]{1,0:T(8,128)(2,1)} %q_hbm.1, bf16[256,512]{1,0:T(8,128)(2,1)} %k_hbm.1, bf16[256,512]{1,0:T(8,128)(2,1)} %v_hbm.1, s32[1,256]{1,0:T(1,128)} %bitcast.1), custom_call_target="tpu_custom_call" | custom-call | tf_op jit(solution)/shard_map/pallas_call | solution.py:483
  39.0 1.3 %copy.8 = bf16[256,4096]{1,0:T(8,128)(2,1)} copy(bf16[256,4096]{1,0:T(8,128)(2,1)S(1)} %get-tuple-element.2) | data formatting | bytes 4194304
  40.3 0.7 %copy.9 = bf16[256,512]{1,0:T(8,128)(2,1)} copy(bf16[256,512]{1,0:T(8,128)(2,1)S(1)} %get-tuple-element.3) | data formatting | bytes 524288

commit v4 on v3

--- a/solution.py
+++ b/solution.py
@@ -16,6 +16,7 @@
 STEP = 16
 SLOTS = SPAN + 2
 LOG2E = 1.4426950408889634
+QUARTER_TURN = 1.5707963267948966
 LOG2_BASE = 19.931568569324174
 
 
@@ -404,8 +405,10 @@
     index = lax.broadcasted_iota(jnp.int32, (rows, 1), 0).astype(jnp.float32)
     positions = index - before + jnp.where(column == lead, earlier, 0.0)
     angles = positions * freq
-    cosine = jnp.cos(angles)
-    sine = jnp.sin(angles) * sign
+    both = jnp.cos(angles - jnp.where(lane < HALF, 0.0, QUARTER_TURN))
+    swapped = pltpu.roll(both, HALF, 1)
+    cosine = jnp.where(lane < HALF, both, swapped)
+    sine = jnp.where(lane < HALF, swapped, both) * sign
     for kv in range(kv_heads):
         at = slice(kv * HD, (kv + 1) * HD)
         x = kraw[0, kv].astype(jnp.float32)

time: 41.3 us -> 41 us (level)
  no operation moved by 1% of the time
where the time goes in v4:
time: 41 us; the launch traced here: 40.8 us
  Pallas kernels  38.1 us (93%)
  local copies, waits for them, and re-layouts  2.02 us (5%)
  between operations  0.64 us (2%)
    pallas_call x1, Pallas kernels, local(): pl.pallas_call(partial(kernel, kv_heads, count), out_shape=(pltpu.VMEM(qu...  38.1 us
    unnamed x2, local copies, waits for them, and re-layouts  2.02 us

profile of v4, /device:TPU:17, one launch (start us, length us, event | category | flops | bytes accessed | tf_op | source)
XLA Modules:
  0.0 40.8 jit_solution(2382032717796690308)
XLA Ops:
  0.6 38.1 %shard_map.59 = (bf16[256,4096]{1,0:T(8,128)(2,1)S(1)}, bf16[256,512]{1,0:T(8,128)(2,1)S(1)}) custom-call(bf16[256,4096]{1,0:T(8,128)(2,1)} %q_hbm.1, bf16[256,512]{1,0:T(8,128)(2,1)} %k_hbm.1, bf16[256,512]{1,0:T(8,128)(2,1)} %v_hbm.1, s32[1,256]{1,0:T(1,128)} %bitcast.1), custom_call_target="tpu_custom_call" | custom-call | tf_op jit(solution)/shard_map/pallas_call | solution.py:486
  38.8 1.3 %copy.8 = bf16[256,4096]{1,0:T(8,128)(2,1)} copy(bf16[256,4096]{1,0:T(8,128)(2,1)S(1)} %get-tuple-element.2) | data formatting | bytes 4194304
  40.1 0.7 %copy.9 = bf16[256,512]{1,0:T(8,128)(2,1)} copy(bf16[256,512]{1,0:T(8,128)(2,1)S(1)} %get-tuple-element.3) | data formatting | bytes 524288
